TPU v7x, 32 devices: a whole 2x2x4 slice. The times are simulated.
32 devices in a mesh: seq: 32 (over z, y, x, core), head: 1.
Axes of the slice: x: 2, y: 2, z: 4, core: 2. Of those that a mesh axis runs over, the one named last changes fastest.
Arguments:
- queries: bfloat16 [8192, 4096], P('seq', 'head'), may hold values from -8 to 8
- keys: bfloat16 [8192, 1024], P('seq', 'head'), may hold values from -8 to 8
- values: bfloat16 [8192, 1024], P('seq', 'head'), may hold values from -8 to 8
- gate_logit: float32 [32], P('head'), may hold values from -3 to 3
- out_weight: bfloat16 [4096, 4096], P('head'), may hold values from -0.09375 to 0.09375
Outputs:
- layer_out: bfloat16 [8192, 4096], P('seq', 'head')
All inputs are finite; a program needn't handle non-finite values.
Results may differ from a plain program's by a relative error of at most 0.0095.
Values may be sent and summed in bfloat16 or wider, within the bound.
A program may use at most 320 MiB of HBM per device.

v0:
```python
import functools
import math

import jax
import jax.numpy as jnp
from jax import lax
from jax.experimental import pallas as pl
from jax.experimental.pallas import tpu as pltpu
from jax.sharding import PartitionSpec as P

HDIM = 128
WINDOW = 4096
SEG = 1024
LOG2E = 1.4426950408889634
EXP_SCALE = LOG2E / math.sqrt(HDIM)


def feature(source):
    wide = source.astype(jnp.float32)
    low = jnp.exp(jnp.minimum(wide, 0.0))
    return jnp.where(wide > 0.0, wide + 1.0, low)


def kernel(
    size, group_size, gate_ref, q_ref, k_hbm, v_hbm, out_ref,
    kbuf, vbuf, m_ref, acc_ref, wsend, wrecv, dsum, dpre,
    local_sem, send_sem, recv_sem, zsend, zrecv, dsend, drecv,
):
    rows = q_ref.shape[0]
    width = kbuf.shape[2]
    groups = width // HDIM
    me = lax.axis_index("seq")
    plane = me // 8
    p = me % 8
    core = p % 2
    xbit = (p // 2) % 2
    ybit = p // 4
    base = me - p
    by_core = 1 - 2 * core
    by_x = 2 - 4 * xbit
    by_y = 4 - 8 * ybit
    dev_core, dev_x, dev_y = me + by_core, me + by_x, me + by_y
    slots = (p, p + by_x, p + by_y, p + by_x + by_y)
    bufs = (kbuf, vbuf)
    X_FIRST = ((True, True), (True, False), (True, False))

    has_up = me + 8 < size
    has_down = plane >= 1

    def rows_of(slot):
        return pl.ds(pl.multiple_of(slot * rows, rows), rows)

    def remote(src, dst, ssem, rsem, dev):
        return pltpu.make_async_remote_copy(
            src_ref=src, dst_ref=dst, send_sem=ssem, recv_sem=rsem,
            device_id={"seq": dev}, device_id_type=pl.DeviceIdType.MESH,
        )

    def hop(g, kv, slot, dev, idx):
        ref = bufs[kv].at[g, rows_of(slot), :]
        return remote(ref, ref, send_sem.at[g, kv, idx], recv_sem.at[g, kv, idx], dev)

    def up(g, kv):
        src = bufs[kv].at[g, rows_of(p), :]
        dst = bufs[kv].at[g + 1, rows_of(p), :]
        return remote(src, dst, zsend.at[g, kv], zrecv.at[g, kv], me + 8)

    def first_step(g, kv):
        return hop(g, kv, slots[0], dev_x if X_FIRST[g][kv] else dev_y, 0)

    def second_step(g, kv, which):
        if X_FIRST[g][kv]:
            return hop(g, kv, slots[(0, 1)[which]], dev_y, 1 + which)
        return hop(g, kv, slots[(0, 2)[which]], dev_x, 1 + which)

    def core_step(g, kv, which):
        return hop(g, kv, slots[which], dev_core, 3 + which)

    def sends_y(g):
        return (ybit == 0, ybit < 2, ybit == 1)[g]

    def far(g):
        return (ybit == 1, ybit < 2, ybit == 0)[g]

    def has(g):
        return plane >= g

    def conds(g, kv, idx):
        y_send, y_recv = has(g) & sends_y(g), has(g) & far(g)
        both = (has(g), has(g))
        if idx == 0:
            return both if X_FIRST[g][kv] else (y_send, y_recv)
        if idx in (1, 2):
            if X_FIRST[g][kv]:
                return (y_send, y_recv)
            return both if idx == 1 else (y_recv, y_recv)
        return both if idx in (3, 4) else (y_recv, y_recv)

    def copy_of(g, kv, idx):
        if idx == 0:
            return first_step(g, kv)
        if idx in (1, 2):
            return second_step(g, kv, idx - 1)
        return core_step(g, kv, idx - 3)

    def start(g, kv, idx):
        @pl.when(conds(g, kv, idx)[0])
        def _():
            copy_of(g, kv, idx).start()

    def arrive(g, kv, idx):
        @pl.when(conds(g, kv, idx)[1])
        def _():
            copy_of(g, kv, idx).wait_recv()

    def exchange(i, value):
        dev = (dev_core, dev_x, dev_y)[i]
        wsend[i] = value.astype(jnp.bfloat16)
        remote(wsend.at[i], wrecv.at[i], dsend.at[i], drecv.at[i], dev).start()

    def exchanged(i):
        dev = (dev_core, dev_x, dev_y)[i]
        remote(wsend.at[i], wrecv.at[i], dsend.at[i], drecv.at[i], dev).wait_recv()
        return wrecv[i].astype(jnp.float32)

    def chain():
        return remote(wsend.at[3], wrecv.at[3], dsend.at[3], drecv.at[3], me + 8)

    def attend(g, chunk, masked=False):
        first_row = pl.multiple_of(chunk * (2 * rows), 2 * rows)
        ones = jnp.ones((2 * rows, HDIM), jnp.bfloat16)
        if masked:
            qpos = lax.broadcasted_iota(jnp.int32, (rows, 2 * rows), 0) + p * rows
            kpos = lax.broadcasted_iota(jnp.int32, (rows, 2 * rows), 1) + first_row
            allowed = (qpos >= kpos) if g == 0 else (kpos > qpos)

        def head(h, carry):
            cols = pl.ds(pl.multiple_of(h * HDIM, HDIM), HDIM)
            k = kbuf[g, pl.ds(first_row, 2 * rows), cols]
            v = vbuf[g, pl.ds(first_row, 2 * rows), cols]
            v_wide = jnp.concatenate([v, ones], axis=1)
            for r in range(group_size):
                n = h * group_size + r
                q = q_ref[:, pl.ds(pl.multiple_of(n * HDIM, HDIM), HDIM)]
                s = lax.dot_general(
                    q, k, (((1,), (1,)), ((), ())), preferred_element_type=jnp.float32
                )
                if masked:
                    s = jnp.where(allowed, s, jnp.float32(-1e30))
                old = m_ref[n]
                new = jnp.maximum(old, jnp.max(s, axis=1, keepdims=True))
                m_ref[n] = new
                alpha = jnp.exp2((old - new) * EXP_SCALE)
                shift = jnp.concatenate([new] * (2 * rows // HDIM), axis=1)
                w = jnp.exp2((s - shift) * EXP_SCALE).astype(jnp.bfloat16)
                pv = jnp.dot(w, v_wide, preferred_element_type=jnp.float32)
                acc_ref[n] = acc_ref[n] * jnp.concatenate([alpha, alpha], axis=1) + pv
            return carry

        lax.fori_loop(0, groups, head, 0)

    own_chunk = p // 2
    near_chunk = own_chunk + 1 - 2 * xbit
    far_base = 2 - 2 * ybit
    KV = (0, 1)

    local = [
        pltpu.make_async_copy(hbm, buf.at[0, rows_of(p), :], local_sem.at[i])
        for i, (hbm, buf) in enumerate(((k_hbm, kbuf), (v_hbm, vbuf)))
    ]
    for c in local:
        c.start()
    barrier = pltpu.get_barrier_semaphore()
    for dev in (dev_core, dev_x, dev_y):
        pl.semaphore_signal(
            barrier, inc=1, device_id={"seq": dev}, device_id_type=pl.DeviceIdType.MESH
        )

    @pl.when(has_up)
    def _():
        pl.semaphore_signal(
            barrier, inc=1, device_id={"seq": me + 8}, device_id_type=pl.DeviceIdType.MESH
        )

    @pl.when(has_down)
    def _():
        pl.semaphore_signal(
            barrier, inc=1, device_id={"seq": me - 8}, device_id_type=pl.DeviceIdType.MESH
        )

    steps = max(size // 8 - 1, 1)
    neighbours_up = 1 - plane // steps if size > 8 else 0
    neighbours_down = (plane + steps - 1) // steps if size > 8 else 0
    pl.semaphore_wait(barrier, 3 + neighbours_up + jnp.minimum(neighbours_down, 1))

    for c in local:
        c.wait()

    for kv in KV:
        start(0, kv, 3)
    for kv in KV:
        @pl.when(has_up)
        def _(kv=kv):
            up(0, kv).start()

        start(0, kv, 0)
    m_ref[...] = jnp.full(m_ref.shape, -1e30, jnp.float32)
    acc_ref[...] = jnp.zeros(acc_ref.shape, jnp.float32)
    for h in range(groups):
        cols = slice(h * HDIM, (h + 1) * HDIM)
        kf = feature(kbuf[0, rows_of(p), cols]).astype(jnp.bfloat16)
        v = vbuf[0, rows_of(p), cols]
        dsum[0:HDIM, cols] = lax.dot_general(
            kf, v, (((0,), (0,)), ((), ())), preferred_element_type=jnp.float32
        )
        norm = jnp.sum(kf.astype(jnp.float32), axis=0, keepdims=True)
        dsum[HDIM:, cols] = jnp.broadcast_to(norm, (dsum.shape[0] - HDIM, HDIM))
    exchange(0, dsum[...])
    for kv in KV:
        arrive(0, kv, 3)
    attend(0, own_chunk, masked=True)
    dsum[...] += exchanged(0)
    exchange(1, dsum[...])

    for kv in KV:
        arrive(0, kv, 0)
        start(0, kv, 4)

    @pl.when(has(1))
    def _():
        for kv in KV:
            up(0, kv).wait_recv()

    for kv in KV:
        start(1, kv, 3)
        start(1, kv, 0)

        @pl.when(has(1) & has_up)
        def _(kv=kv):
            up(1, kv).start()

    for kv in KV:
        arrive(0, kv, 4)

    @pl.when(xbit == 1)
    def _():
        attend(0, near_chunk)

    for kv in KV:
        arrive(1, kv, 3)

    @pl.when(has(1))
    def _():
        attend(1, own_chunk)

    dsum[...] += exchanged(1)
    exchange(2, dsum[...])

    for kv in KV:
        arrive(1, kv, 0)
        start(1, kv, 1)
        start(1, kv, 2)
        start(1, kv, 4 if X_FIRST[1][kv] else 5)
    for kv in KV:
        start(0, kv, 1)
        start(0, kv, 2)

    @pl.when(has(2))
    def _():
        for kv in KV:
            up(1, kv).wait_recv()

    for kv in KV:
        start(2, kv, 3)
        start(2, kv, 0)
    other = exchanged(2)
    dpre[...] = other * ybit.astype(jnp.float32)
    dsum[...] += other

    @pl.when(has_up & (plane == 0))
    def _():
        wsend[3] = dsum[...].astype(jnp.bfloat16)
        chain().start()

    for kv in KV:
        arrive(2, kv, 3)

    @pl.when(has(2))
    def _():
        attend(2, own_chunk, masked=True)

    @pl.when(has_down)
    def _():
        chain().wait_recv()
        before = wrecv[3].astype(jnp.float32)
        dpre[...] += before

        @pl.when(has_up)
        def _():
            wsend[3] = (before + dsum[...]).astype(jnp.bfloat16)
            chain().start()

    for kv in KV:
        arrive(1, kv, 1)
        arrive(1, kv, 2)
        start(1, kv, 5 if X_FIRST[1][kv] else 4)
        start(1, kv, 6)
    for kv in KV:
        arrive(2, kv, 0)
        start(2, kv, 1)
        start(2, kv, 2)
        start(2, kv, 4 if X_FIRST[2][kv] else 5)
    for kv in KV:
        arrive(1, kv, 4)
        arrive(1, kv, 5)
        arrive(1, kv, 6)

    @pl.when(has(1))
    def _():
        def one(i, c):
            attend(1, (own_chunk + 1 + i) % 4)
            return c

        lax.fori_loop(0, 3, one, 0)

    for kv in KV:
        arrive(2, kv, 1)
        arrive(2, kv, 2)
        start(2, kv, 5 if X_FIRST[2][kv] else 4)
        start(2, kv, 6)
    for kv in KV:
        arrive(2, kv, 4)
        arrive(2, kv, 5)
        arrive(2, kv, 6)

    @pl.when(has(2) & (xbit == 0))
    def _():
        attend(2, near_chunk)

    for kv in KV:
        arrive(0, kv, 1)
        arrive(0, kv, 2)
        start(0, kv, 5)
        start(0, kv, 6)
    for kv in KV:
        arrive(0, kv, 5)
        arrive(0, kv, 6)

    @pl.when(far(0))
    def _():
        lax.fori_loop(0, 2, lambda i, c: (attend(0, far_base + i), c)[1], 0)

    @pl.when(has(2) & far(2))
    def _():
        lax.fori_loop(0, 2, lambda i, c: (attend(2, far_base + i), c)[1], 0)

    def finish(h, carry):
        cols = pl.ds(pl.multiple_of(h * HDIM, HDIM), HDIM)
        mem = dpre[0:HDIM, cols]
        high = mem.astype(jnp.bfloat16)
        low = (mem - high.astype(jnp.float32)).astype(jnp.bfloat16)
        norm = dpre[HDIM:HDIM + 1, cols]
        for r in range(group_size):
            n = h * group_size + r
            qcols = pl.ds(pl.multiple_of(n * HDIM, HDIM), HDIM)
            qf = feature(q_ref[:, qcols]).astype(jnp.bfloat16)
            recalled = jnp.dot(qf, high, preferred_element_type=jnp.float32) + jnp.dot(
                qf, low, preferred_element_type=jnp.float32
            )
            denominator = 1.0 + jnp.sum(qf.astype(jnp.float32) * norm, axis=1, keepdims=True)
            local_out = acc_ref[n, :, 0:HDIM] / acc_ref[n, :, HDIM:]
            share = gate_ref[n]
            mixed = share * (recalled / denominator) + (1.0 - share) * local_out
            out_ref[:, qcols] = mixed.astype(jnp.bfloat16)
        return carry

    lax.fori_loop(0, groups, finish, 0)

    for i, dev in enumerate((dev_core, dev_x, dev_y)):
        remote(wsend.at[i], wrecv.at[i], dsend.at[i], drecv.at[i], dev).wait_send()

    @pl.when(has_up)
    def _():
        chain().wait_send()
        for kv in KV:
            up(0, kv).wait_send()

    @pl.when(has_up & has(1))
    def _():
        for kv in KV:
            up(1, kv).wait_send()

    for g in range(3):
        for kv in KV:
            for idx in range(7):
                @pl.when(conds(g, kv, idx)[0])
                def _(g=g, kv=kv, idx=idx):
                    copy_of(g, kv, idx).wait_send()


def per_device(size, queries, keys, values, gate_logit, out_weight):
    rows = queries.shape[0]
    heads = gate_logit.shape[0]
    width = keys.shape[1]
    group_size = heads // (width // HDIM)
    assert WINDOW == 16 * rows and SEG == 4 * rows and size % 8 == 0
    vmem, anywhere = pl.BlockSpec(memory_space=pltpu.VMEM), pl.BlockSpec(memory_space=pl.ANY)
    mixed = pl.pallas_call(
        functools.partial(kernel, size, group_size),
        out_shape=jax.ShapeDtypeStruct(queries.shape, jnp.bfloat16),
        in_specs=[pl.BlockSpec(memory_space=pltpu.SMEM), vmem, anywhere, anywhere],
        out_specs=vmem,
        scratch_shapes=[
            pltpu.VMEM((3, 8 * rows, width), jnp.bfloat16),
            pltpu.VMEM((3, 8 * rows, width), jnp.bfloat16),
            pltpu.VMEM((heads, rows, HDIM), jnp.float32),
            pltpu.VMEM((heads, rows, 2 * HDIM), jnp.float32),
            pltpu.VMEM((4, HDIM + 16, width), jnp.bfloat16),
            pltpu.VMEM((4, HDIM + 16, width), jnp.bfloat16),
            pltpu.VMEM((HDIM + 16, width), jnp.float32),
            pltpu.VMEM((HDIM + 16, width), jnp.float32),
            pltpu.SemaphoreType.DMA((2,)),
            pltpu.SemaphoreType.DMA((3, 2, 7)),
            pltpu.SemaphoreType.DMA((3, 2, 7)),
            pltpu.SemaphoreType.DMA((2, 2)),
            pltpu.SemaphoreType.DMA((2, 2)),
            pltpu.SemaphoreType.DMA((4,)),
            pltpu.SemaphoreType.DMA((4,)),
        ],
        compiler_params=pltpu.CompilerParams(
            collective_id=0, has_side_effects=True, vmem_limit_bytes=60 * 1024 * 1024
        ),
    )(jax.nn.sigmoid(gate_logit), queries, keys, values)
    partial_value = jnp.dot(mixed, out_weight, preferred_element_type=jnp.float32)
    return lax.psum_scatter(
        partial_value.astype(jnp.bfloat16), "head", scatter_dimension=1, tiled=True
    )


def solution(mesh):
    in_specs = (P("seq", "head"), P("seq", "head"), P("seq", "head"), P("head"), P("head", None))
    out_specs = P("seq", "head")
    return jax.shard_map(
        functools.partial(per_device, mesh.shape["seq"]),
        mesh=mesh, in_specs=in_specs, out_specs=out_specs, check_vma=False,
    )
```

profile of v0, /device:TPU:24, one launch (start us, length us, event | category | flops | bytes accessed | tf_op | source)
XLA Modules:
  0.0 161.2 jit_solution(14804708225440435335)
XLA Ops:
  0.0 1.2 add_divide_fusion.gate_ref
  1.2 143.4 %shard_map.55 = bf16[256,4096]{1,0:T(8,128)(2,1)} custom-call(f32[32]{0:T(128)} %add_divide_fusion.gate_ref, bf16[256,4096]{1,0:T(8,128)(2,1)} %q_ref.1, bf16[256,1024]{1,0:T(8,128)(2,1)} %k_hbm.1, bf16[256,1024]{1,0:T(8,128)(2,1)} %v_hbm.1), custom_call_target="tpu_custom_call" | custom-call | tf_op jit(solution)/shard_map/pallas_call | solution.py:408
  144.6 16.6 %convolution_convert_fusion = bf16[256,4096]{1,0:T(8,128)(2,1)} fusion(bf16[256,4096]{1,0:T(8,128)(2,1)} %shard_map.55, bf16[4096,4096]{1,0:T(8,128)(2,1)} %param.9), kind=kOutput, calls=%fused_computation | convolution fusion | flops 8590983168 | bytes 37748736 | tf_op jit(solution)/shard_map/dot_general | solution.py:434
where the time goes:
time: 162 us; the launch traced here: 161 us
  Pallas kernels  143 us (88%)
  matrix products  16.6 us (10%)
    pallas_call x1, Pallas kernels, per_device(): pl.pallas_call(functools.partial(kernel, size, group_size), out_shape=jax...  143 us
    dot_general x1, matrix products, per_device(): jnp.dot(mixed, out_weight, preferred_element_type=jnp.float32)  16.6 us

commit v1 on v0

v1 whole, which is shorter than its diff:
```python
import functools
import math

import jax
import jax.numpy as jnp
from jax import lax
from jax.experimental import pallas as pl
from jax.experimental.pallas import tpu as pltpu
from jax.sharding import PartitionSpec as P

HDIM = 128
WINDOW = 4096
SEG = 1024
LOG2E = 1.4426950408889634
EXP_SCALE = LOG2E / math.sqrt(HDIM)
TILE = 512
PAD = 16
ZB, ZC, BX, BY, BYF, AX, AY, AXF = range(8)
KV = (0, 1)


def feature(source):
    wide = source.astype(jnp.float32)
    low = jnp.exp(jnp.minimum(wide, 0.0))
    return jnp.where(wide > 0.0, wide + 1.0, low)


def kernel(
    size, group_size, gate_ref, q_hbm, k_hbm, v_hbm, w_hbm, out_ref,
    qbuf, kbuf, vbuf, m_ref, acc_ref, mix, wbuf, psend, precv, pown,
    wsend, wrecv, dsum, dpre,
    local_sem, xsend, xrecv, send_sem, recv_sem, dsend, drecv, psem, prsem,
):
    rows = q_hbm.shape[0]
    heads = kbuf.shape[0]
    width = heads * HDIM
    qwidth = width * group_size
    own_q = heads * group_size
    blocks = 2 * group_size
    tiles = w_hbm.shape[1] // TILE
    me = lax.axis_index("seq")
    plane = me // 8
    p = me % 8
    core = p % 2
    xbit = (p // 2) % 2
    ybit = p // 4
    j = p // 2
    j_x = j + 1 - 2 * xbit
    j_y = j + 2 - 4 * ybit
    dev_core = me + 1 - 2 * core
    dev_x = me + 2 - 4 * xbit
    dev_y = me + 4 - 8 * ybit
    bufs = (kbuf, vbuf)
    has_up = me + 8 < size
    has_down = plane >= 1
    two_down = plane >= 2

    def remote(src, dst, ssem, rsem, dev):
        return pltpu.make_async_remote_copy(
            src_ref=src, dst_ref=dst, send_sem=ssem, recv_sem=rsem,
            device_id={"seq": dev}, device_id_type=pl.DeviceIdType.MESH,
        )

    plan = {
        ZB: (j, 4 + j, me + 8, has_up, has_down),
        ZC: (4 + j, 8, me + 8, has_up & has_down, two_down),
        BX: (4 + j, 4 + j, dev_x, has_down, has_down),
        BY: (4 + j, 4 + j, dev_y, has_down, has_down),
        BYF: (4 + j_x, 4 + j_x, dev_y, has_down, has_down),
        AX: (j + xbit * (8 - j), j, dev_x, (xbit == 0) | two_down, (xbit == 1) | two_down),
        AY: (j + ybit * (8 - j), j, dev_y, (ybit == 0) | two_down, (ybit == 1) | two_down),
        AXF: (j_y, j_y, dev_x, (ybit == 1) | two_down, (ybit == 1) | two_down),
    }

    def copy_of(kind, h, kv):
        src, dst, dev, _, _ = plan[kind]
        return remote(
            bufs[kv].at[h, src], bufs[kv].at[h, dst],
            send_sem.at[kind, h, kv], recv_sem.at[kind, h, kv], dev,
        )

    def start(kind, h, also=None):
        ok = plan[kind][3] if also is None else plan[kind][3] & also

        @pl.when(ok)
        def _():
            for kv in KV:
                copy_of(kind, h, kv).start()

    def arrive(kind, h):
        @pl.when(plan[kind][4])
        def _():
            for kv in KV:
                copy_of(kind, h, kv).wait_recv()

    def event_0(h):
        start(ZB, h)
        start(AX, h, xbit == 0)
        start(AY, h, ybit == 0)

    def event_1(h):
        arrive(ZB, h)
        start(BX, h)
        start(BY, h)
        start(ZC, h)

    def event_2(h):
        arrive(ZC, h)
        start(AX, h, xbit == 1)
        start(AY, h, ybit == 1)

    def event_3(h):
        arrive(BX, h)
        start(BYF, h)

    def event_4(h):
        arrive(AY, h)
        start(AXF, h)

    def when_head(h, event):
        @pl.when(h < heads)
        def _():
            event(h)

    def delta_copy(i):
        dev = (dev_x, dev_y, me + 8)[i]
        return remote(wsend.at[i], wrecv.at[i], dsend.at[i], drecv.at[i], dev)

    def delta_send(i, value):
        wsend[i] = value.astype(jnp.bfloat16)
        delta_copy(i).start()

    def delta_arrive(i):
        delta_copy(i).wait_recv()
        return wrecv[i].astype(jnp.float32)

    def attend(h, slot, mask=None):
        qk_dims = (((1,), (1,)), ((), ()))

        def span(half):
            if mask == "own" and half == 0:
                return 0, rows
            if mask == "old" and half == 1:
                return rows, rows
            return 0, 2 * rows

        def block(i):
            return slice(i * rows, (i + 1) * rows)

        def scores(i):
            first, count = span(i % 2)
            cols = pl.ds(pl.multiple_of((h * group_size + i // 2) * HDIM, HDIM), HDIM)
            q = qbuf[(i % 2) * rows:(i % 2 + 1) * rows, cols]
            s = lax.dot_general(
                q, kbuf[h, slot, first:first + count, :], qk_dims,
                preferred_element_type=jnp.float32,
            )
            if mask is None:
                return s
            qpos = lax.broadcasted_iota(jnp.int32, (rows, rows), 0)
            kpos = lax.broadcasted_iota(jnp.int32, (rows, rows), 1)
            allowed = (qpos >= kpos) if mask == "own" else (kpos > qpos)
            low = jnp.float32(-1e30)
            if count == rows:
                return jnp.where(allowed, s, low)
            if mask == "own":
                return jnp.concatenate([s[:, :rows], jnp.where(allowed, s[:, rows:], low)], axis=1)
            return jnp.concatenate([jnp.where(allowed, s[:, :rows], low), s[:, rows:]], axis=1)

        def soften(i, s):
            top = jnp.max(s, axis=1, keepdims=True)
            shape = (rows, HDIM)
            if mask == "own":
                new, alpha = jnp.broadcast_to(top, shape), None
            else:
                old = m_ref[block(i), :]
                new = jnp.maximum(old, top)
                alpha = jnp.exp2((old - new) * EXP_SCALE)
            m_ref[block(i), :] = new
            shift = jnp.concatenate([new] * (s.shape[1] // HDIM), axis=1)
            return jnp.exp2((s - shift) * EXP_SCALE).astype(jnp.bfloat16), alpha

        def gather(i, w, alpha):
            first, count = span(i % 2)
            v = vbuf[h, slot, first:first + count, :]
            wide = jnp.concatenate([v, jnp.ones((count, HDIM), jnp.bfloat16)], axis=1)
            pv = jnp.dot(w, wide, preferred_element_type=jnp.float32)
            if alpha is None:
                acc_ref[block(i), :] = pv
            else:
                acc_ref[block(i), :] = (
                    acc_ref[block(i), :] * jnp.concatenate([alpha, alpha], axis=1) + pv
                )

        waiting, ready = {}, {}
        for t in range(blocks + 2):
            if t < blocks:
                waiting[t] = scores(t)
            if 0 <= t - 1 < blocks:
                ready[t - 1] = soften(t - 1, waiting.pop(t - 1))
            if 0 <= t - 2 < blocks:
                gather(t - 2, *ready.pop(t - 2))

    def finish(h):
        cols = pl.ds(pl.multiple_of(h * HDIM, HDIM), HDIM)
        mem = dpre[0:HDIM, cols]
        high = mem.astype(jnp.bfloat16)
        low = (mem - high.astype(jnp.float32)).astype(jnp.bfloat16)
        norm = dpre[HDIM:HDIM + 1, cols]

        def one(r, carry):
            n = h * group_size + r
            qcols = pl.ds(pl.multiple_of(n * HDIM, HDIM), HDIM)
            arows = pl.ds(pl.multiple_of(r * (2 * rows), 2 * rows), 2 * rows)
            qf = feature(qbuf[:, qcols]).astype(jnp.bfloat16)
            recalled = jnp.dot(qf, high, preferred_element_type=jnp.float32) + jnp.dot(
                qf, low, preferred_element_type=jnp.float32
            )
            denominator = 1.0 + jnp.sum(qf.astype(jnp.float32) * norm, axis=1, keepdims=True)
            local_out = acc_ref[arows, 0:HDIM] / acc_ref[arows, HDIM:]
            share = gate_ref[core * own_q + n]
            mixed = share * (recalled / denominator) + (1.0 - share) * local_out
            mix[:, qcols] = mixed.astype(jnp.bfloat16)
            return carry

        lax.fori_loop(0, group_size, one, 0)

    mine = pl.ds(pl.multiple_of(core * rows, rows), rows)
    hbms = (k_hbm, v_hbm)

    def head_cols(owner, h):
        return pl.ds(pl.multiple_of((owner * heads + h) * HDIM, HDIM), HDIM)

    def half_cols(owner):
        return pl.ds(pl.multiple_of(owner * qwidth, qwidth), qwidth)

    local, swaps = [], []
    for h in range(heads):
        for kv in KV:
            i = 2 * h + kv
            place = bufs[kv].at[h, j, mine, :]
            local.append(pltpu.make_async_copy(
                hbms[kv].at[:, head_cols(core, h)], place, local_sem.at[i]))
            swaps.append(remote(
                hbms[kv].at[:, head_cols(1 - core, h)], place, xsend.at[i], xrecv.at[i], dev_core))
    local.append(pltpu.make_async_copy(
        q_hbm.at[:, half_cols(core)], qbuf.at[mine, :], local_sem.at[2 * heads]))
    swaps.append(remote(
        q_hbm.at[:, half_cols(1 - core)], qbuf.at[mine, :],
        xsend.at[2 * heads], xrecv.at[2 * heads], dev_core))
    weights = pltpu.make_async_copy(
        w_hbm.at[pl.ds(pl.multiple_of(core * qwidth, qwidth), qwidth), :], wbuf,
        local_sem.at[2 * heads + 1])

    for c in local:
        c.start()
    barrier = pltpu.get_barrier_semaphore()
    for dev in (dev_core, dev_x, dev_y):
        pl.semaphore_signal(
            barrier, inc=1, device_id={"seq": dev}, device_id_type=pl.DeviceIdType.MESH
        )

    @pl.when(has_up)
    def _():
        pl.semaphore_signal(
            barrier, inc=1, device_id={"seq": me + 8}, device_id_type=pl.DeviceIdType.MESH
        )

    @pl.when(has_down)
    def _():
        pl.semaphore_signal(
            barrier, inc=1, device_id={"seq": me - 8}, device_id_type=pl.DeviceIdType.MESH
        )

    steps = max(size // 8 - 1, 1)
    neighbours_up = 1 - plane // steps if size > 8 else 0
    neighbours_down = (plane + steps - 1) // steps if size > 8 else 0
    pl.semaphore_wait(barrier, 3 + neighbours_up + jnp.minimum(neighbours_down, 1))

    for c in swaps:
        c.start()
    weights.start()
    for c in local:
        c.wait()
    for c in swaps:
        c.wait_recv()

    event_0(0)
    for h in range(heads):
        cols = slice(h * HDIM, (h + 1) * HDIM)
        kf = feature(kbuf[h, j]).astype(jnp.bfloat16)
        dsum[0:HDIM, cols] = lax.dot_general(
            kf, vbuf[h, j], (((0,), (0,)), ((), ())), preferred_element_type=jnp.float32
        )
        norm = jnp.sum(kf.astype(jnp.float32), axis=0, keepdims=True)
        dsum[HDIM:, cols] = jnp.broadcast_to(norm, (PAD, HDIM))
    delta_send(0, dsum[...])
    event_1(0)
    event_0(1)
    dsum[...] += delta_arrive(0)
    delta_send(1, dsum[...])
    event_2(0)
    event_3(0)
    other = delta_arrive(1)
    dpre[...] = other * ybit.astype(jnp.float32)
    dsum[...] += other

    @pl.when(has_up & (plane == 0))
    def _():
        delta_send(2, dsum[...])

    event_4(0)

    def chain():
        @pl.when(has_down)
        def _():
            before = delta_arrive(2)
            dpre[...] += before

            @pl.when(has_up)
            def _():
                delta_send(2, before + dsum[...])

    def xor(a_bit, b_bit):
        return a_bit + b_bit - 2 * a_bit * b_bit

    def one_head(h, carry):
        attend(h, j, "own")
        when_head(h + 1, event_1)

        def step(s, c):
            late = s // 4
            t = s - 3 * late
            slot = 4 * (1 - late) + xor(xbit, t % 2) + 2 * xor(ybit, t // 2)

            @pl.when(s == 1)
            def _():
                when_head(h + 2, event_0)

            @pl.when(s == 2)
            def _():
                arrive(BY, h)

            @pl.when(s == 3)
            def _():
                when_head(h + 1, event_2)
                when_head(h + 1, event_3)
                arrive(BYF, h)

                @pl.when(h == 0)
                def _():
                    chain()

            @pl.when(s == 4)
            def _():
                arrive(AX, h)

            @pl.when(s == 5)
            def _():
                when_head(h + 1, event_4)

            @pl.when(s == 6)
            def _():
                arrive(AXF, h)

            bit = jnp.where(s == 4, xbit, ybit)
            valid = ((s < 4) & has_down) | ((s >= 4) & ((bit == 1) | two_down))

            @pl.when(valid)
            def _():
                attend(h, slot)

            return c

        lax.fori_loop(0, 7, step, 0)

        @pl.when(two_down)
        def _():
            attend(h, 8, "old")

        finish(h)
        return carry

    lax.fori_loop(0, heads, one_head, 0)

    weights.wait()
    theirs = pl.ds(pl.multiple_of((1 - core) * rows, rows), rows)

    def partial_copy(i):
        return remote(psend.at[i], precv.at[i], psem.at[i], prsem.at[i], dev_core)

    def project(i, carry):
        cols = pl.ds(pl.multiple_of(i * TILE, TILE), TILE)
        psend[i] = jnp.dot(mix[theirs, :], wbuf[:, cols], preferred_element_type=jnp.float32)
        partial_copy(i).start()
        return carry

    def project_own(i, carry):
        cols = pl.ds(pl.multiple_of(i * TILE, TILE), TILE)
        pown[...] = jnp.dot(mix[mine, :], wbuf[:, cols], preferred_element_type=jnp.float32)
        partial_copy(i).wait_recv()
        out_ref[:, cols] = (pown[...] + precv[i]).astype(jnp.bfloat16)
        return carry

    lax.fori_loop(0, tiles, project, 0)
    lax.fori_loop(0, tiles, project_own, 0)

    def sent(i, carry):
        partial_copy(i).wait_send()
        return carry

    lax.fori_loop(0, tiles, sent, 0)
    for c in swaps:
        c.wait_send()
    for i in (0, 1):
        delta_copy(i).wait_send()

    @pl.when(has_up)
    def _():
        delta_copy(2).wait_send()

    def all_sent(h, carry):
        for kind in plan:
            @pl.when(plan[kind][3])
            def _(kind=kind):
                for kv in KV:
                    copy_of(kind, h, kv).wait_send()
        return carry

    lax.fori_loop(0, heads, all_sent, 0)


def per_device(size, queries, keys, values, gate_logit, out_weight):
    rows = queries.shape[0]
    heads = gate_logit.shape[0]
    groups = keys.shape[1] // HDIM
    group_size = heads // groups
    assert WINDOW == 16 * rows and SEG == 4 * rows and size % 8 == 0 and groups % 2 == 0
    mine = groups // 2
    columns = out_weight.shape[1]
    qwidth = mine * group_size * HDIM
    tiles = columns // TILE
    f32, bf16 = jnp.float32, jnp.bfloat16
    vmem, anywhere = pl.BlockSpec(memory_space=pltpu.VMEM), pl.BlockSpec(memory_space=pl.ANY)
    dma = pltpu.SemaphoreType.DMA
    partial_value = pl.pallas_call(
        functools.partial(kernel, size, group_size),
        out_shape=jax.ShapeDtypeStruct((rows, columns), bf16),
        in_specs=[pl.BlockSpec(memory_space=pltpu.SMEM)] + [anywhere] * 4,
        out_specs=vmem,
        scratch_shapes=[
            pltpu.VMEM((2 * rows, qwidth), bf16),
            pltpu.VMEM((mine, 9, 2 * rows, HDIM), bf16),
            pltpu.VMEM((mine, 9, 2 * rows, HDIM), bf16),
            pltpu.VMEM((2 * rows * group_size, HDIM), f32),
            pltpu.VMEM((2 * rows * group_size, 2 * HDIM), f32),
            pltpu.VMEM((2 * rows, qwidth), bf16),
            pltpu.VMEM((qwidth, columns), bf16),
            pltpu.VMEM((tiles, rows, TILE), f32),
            pltpu.VMEM((tiles, rows, TILE), f32),
            pltpu.VMEM((rows, TILE), f32),
            pltpu.VMEM((3, HDIM + PAD, mine * HDIM), bf16),
            pltpu.VMEM((3, HDIM + PAD, mine * HDIM), bf16),
            pltpu.VMEM((HDIM + PAD, mine * HDIM), f32),
            pltpu.VMEM((HDIM + PAD, mine * HDIM), f32),
            dma((2 * mine + 2,)),
            dma((2 * mine + 1,)),
            dma((2 * mine + 1,)),
            dma((8, mine, 2)),
            dma((8, mine, 2)),
            dma((3,)),
            dma((3,)),
            dma((tiles,)),
            dma((tiles,)),
        ],
        compiler_params=pltpu.CompilerParams(
            collective_id=0, has_side_effects=True, vmem_limit_bytes=60 * 1024 * 1024
        ),
    )(jax.nn.sigmoid(gate_logit), queries, keys, values, out_weight)
    return lax.psum_scatter(partial_value, "head", scatter_dimension=1, tiled=True)


def solution(mesh):
    in_specs = (P("seq", "head"), P("seq", "head"), P("seq", "head"), P("head"), P("head", None))
    out_specs = P("seq", "head")
    return jax.shard_map(
        functools.partial(per_device, mesh.shape["seq"]),
        mesh=mesh, in_specs=in_specs, out_specs=out_specs, check_vma=False,
    )
```

time: 162 us -> 132 us (0.81)
  matrix products: 16.6 us -> 0 us
  Pallas kernels: 143 us -> 127 us
  local copies, waits for them, and re-layouts: 0 us -> 3.13 us
    dot_general x1 -> x0, matrix products: 16.6 us -> none  [per_device(): jnp.dot(mixed, out_weight, preferred_element_type=jnp.float32)]
    pallas_call x1, Pallas kernels: 143 us -> 127 us  [per_device(): pl.pallas_call(functools.partial(kernel, size, group_size), out_shape=jax...]
    unnamed x0 -> x1, local copies, waits for them, and re-layouts: none -> 3.13 us
where the time goes in v1:
time: 132 us
  Pallas kernels  127 us (96%)
  local copies, waits for them, and re-layouts  3.13 us (2%)
    pallas_call x1, Pallas kernels, per_device(): pl.pallas_call(functools.partial(kernel, size, group_size), out_shape=jax...  127 us
    unnamed x1, local copies, waits for them, and re-layouts  3.13 us

profile of v1, /device:TPU:24, one launch (start us, length us, event | category | flops | bytes accessed | tf_op | source)
XLA Modules:
  0.0 131.5 jit_solution(15990498686480729901)
XLA Ops:
  0.0 1.2 add_divide_fusion.gate_ref
  1.2 127.2 %shard_map.55 = bf16[256,4096]{1,0:T(8,128)(2,1)} custom-call(f32[32]{0:T(128)} %add_divide_fusion.gate_ref, bf16[256,4096]{1,0:T(8,128)(2,1)} %q_hbm.1, bf16[256,1024]{1,0:T(8,128)(2,1)} %k_hbm.1, bf16[256,1024]{1,0:T(8,128)(2,1)} %v_hbm.1, bf16[4096,4096]{1,0:T(8,128)(2,1)} %w_hbm.1), custom_call_target="tpu_custom_call" | custom-call | tf_op jit(solution)/shard_map/pallas_call | solution.py:446
  128.4 3.1 %copy.7 = bf16[256,4096]{1,0:T(8,128)(2,1)} copy(bf16[256,4096]{1,0:T(8,128)(2,1)} %shard_map.55) | data formatting | bytes 4194304

commit v2 on v1

--- a/solution.py
+++ b/solution.py
@@ -13,7 +13,7 @@
 SEG = 1024
 LOG2E = 1.4426950408889634
 EXP_SCALE = LOG2E / math.sqrt(HDIM)
-TILE = 512
+TILE = 1024
 PAD = 16
 ZB, ZC, BX, BY, BYF, AX, AY, AXF = range(8)
 KV = (0, 1)
@@ -27,13 +27,14 @@
 
 def kernel(
     size, group_size, gate_ref, q_hbm, k_hbm, v_hbm, w_hbm, out_ref,
-    qbuf, kbuf, vbuf, m_ref, acc_ref, mix, wbuf, psend, precv, pown,
+    qbuf, kbuf, vbuf, m_ref, acc_ref, mix, msend, wbuf, pown,
     wsend, wrecv, dsum, dpre,
-    local_sem, xsend, xrecv, send_sem, recv_sem, dsend, drecv, psem, prsem,
+    local_sem, xsend, xrecv, send_sem, recv_sem, dsend, drecv, psem, prsem, wsem,
 ):
     rows = q_hbm.shape[0]
     heads = kbuf.shape[0]
     width = heads * HDIM
+    gwidth = group_size * HDIM
     qwidth = width * group_size
     own_q = heads * group_size
     blocks = 2 * group_size
@@ -79,43 +80,29 @@
             send_sem.at[kind, h, kv], recv_sem.at[kind, h, kv], dev,
         )
 
-    def start(kind, h, also=None):
+    def start(kind, h, also=None, kvs=KV):
         ok = plan[kind][3] if also is None else plan[kind][3] & also
 
         @pl.when(ok)
         def _():
-            for kv in KV:
+            for kv in kvs:
                 copy_of(kind, h, kv).start()
 
-    def arrive(kind, h):
+    def arrive(kind, h, kvs=KV):
         @pl.when(plan[kind][4])
         def _():
-            for kv in KV:
+            for kv in kvs:
                 copy_of(kind, h, kv).wait_recv()
 
-    def event_0(h):
-        start(ZB, h)
-        start(AX, h, xbit == 0)
-        start(AY, h, ybit == 0)
-
-    def event_1(h):
-        arrive(ZB, h)
-        start(BX, h)
-        start(BY, h)
-        start(ZC, h)
-
-    def event_2(h):
+    def relay(kind, onward, h):
+        for kv in KV:
+            arrive(kind, h, (kv,))
+            start(onward, h, None, (kv,))
+
+    def open_head(h):
         arrive(ZC, h)
-        start(AX, h, xbit == 1)
-        start(AY, h, ybit == 1)
-
-    def event_3(h):
-        arrive(BX, h)
-        start(BYF, h)
-
-    def event_4(h):
-        arrive(AY, h)
-        start(AXF, h)
+        for kind in (BX, AY, AX, BY):
+            start(kind, h)
 
     def when_head(h, event):
         @pl.when(h < heads)
@@ -134,7 +121,7 @@
         delta_copy(i).wait_recv()
         return wrecv[i].astype(jnp.float32)
 
-    def attend(h, slot, mask=None):
+    def attend(h, slots, mask=None):
         qk_dims = (((1,), (1,)), ((), ()))
 
         def span(half):
@@ -151,12 +138,16 @@
             first, count = span(i % 2)
             cols = pl.ds(pl.multiple_of((h * group_size + i // 2) * HDIM, HDIM), HDIM)
             q = qbuf[(i % 2) * rows:(i % 2 + 1) * rows, cols]
-            s = lax.dot_general(
-                q, kbuf[h, slot, first:first + count, :], qk_dims,
-                preferred_element_type=jnp.float32,
-            )
+            parts = [
+                lax.dot_general(
+                    q, kbuf[h, slot, first:first + count, :], qk_dims,
+                    preferred_element_type=jnp.float32,
+                )
+                for slot in slots
+            ]
             if mask is None:
-                return s
+                return jnp.concatenate(parts, axis=1) if len(parts) > 1 else parts[0]
+            s, = parts
             qpos = lax.broadcasted_iota(jnp.int32, (rows, rows), 0)
             kpos = lax.broadcasted_iota(jnp.int32, (rows, rows), 1)
             allowed = (qpos >= kpos) if mask == "own" else (kpos > qpos)
@@ -182,14 +173,19 @@
 
         def gather(i, w, alpha):
             first, count = span(i % 2)
-            v = vbuf[h, slot, first:first + count, :]
-            wide = jnp.concatenate([v, jnp.ones((count, HDIM), jnp.bfloat16)], axis=1)
-            pv = jnp.dot(w, wide, preferred_element_type=jnp.float32)
+            pv = None
+            for k, slot in enumerate(slots):
+                v = vbuf[h, slot, first:first + count, :]
+                wide = jnp.concatenate([v, jnp.ones((count, HDIM), jnp.bfloat16)], axis=1)
+                one = jnp.dot(
+                    w[:, k * count:(k + 1) * count], wide, preferred_element_type=jnp.float32
+                )
+                pv = one if pv is None else pv + one
             if alpha is None:
-                acc_ref[block(i), :] = pv
+                acc_ref[h % 2, block(i), :] = pv
             else:
-                acc_ref[block(i), :] = (
-                    acc_ref[block(i), :] * jnp.concatenate([alpha, alpha], axis=1) + pv
+                acc_ref[h % 2, block(i), :] = (
+                    acc_ref[h % 2, block(i), :] * jnp.concatenate([alpha, alpha], axis=1) + pv
                 )
 
         waiting, ready = {}, {}
@@ -208,22 +204,81 @@
         low = (mem - high.astype(jnp.float32)).astype(jnp.bfloat16)
         norm = dpre[HDIM:HDIM + 1, cols]
 
-        def one(r, carry):
-            n = h * group_size + r
-            qcols = pl.ds(pl.multiple_of(n * HDIM, HDIM), HDIM)
-            arows = pl.ds(pl.multiple_of(r * (2 * rows), 2 * rows), 2 * rows)
-            qf = feature(qbuf[:, qcols]).astype(jnp.bfloat16)
-            recalled = jnp.dot(qf, high, preferred_element_type=jnp.float32) + jnp.dot(
-                qf, low, preferred_element_type=jnp.float32
-            )
-            denominator = 1.0 + jnp.sum(qf.astype(jnp.float32) * norm, axis=1, keepdims=True)
-            local_out = acc_ref[arows, 0:HDIM] / acc_ref[arows, HDIM:]
-            share = gate_ref[core * own_q + n]
-            mixed = share * (recalled / denominator) + (1.0 - share) * local_out
-            mix[:, qcols] = mixed.astype(jnp.bfloat16)
+        def part(place, target):
+            def one(r, carry):
+                n = h * group_size + r
+                qcols = pl.ds(pl.multiple_of(n * HDIM, HDIM), HDIM)
+                arows = pl.ds(pl.multiple_of((2 * r + place) * rows, rows), rows)
+                qrows = pl.ds(pl.multiple_of(place * rows, rows), rows)
+                qf = feature(qbuf[qrows, qcols]).astype(jnp.bfloat16)
+                recalled = jnp.dot(qf, high, preferred_element_type=jnp.float32) + jnp.dot(
+                    qf, low, preferred_element_type=jnp.float32
+                )
+                denominator = 1.0 + jnp.sum(qf.astype(jnp.float32) * norm, axis=1, keepdims=True)
+                local_out = acc_ref[h % 2, arows, 0:HDIM] / acc_ref[h % 2, arows, HDIM:]
+                share = jax.nn.sigmoid(jnp.full((1, HDIM), gate_ref[core * own_q + n], jnp.float32))
+                mixed = share * (recalled / denominator) + (1.0 - share) * local_out
+                target[:, pl.ds(pl.multiple_of(r * HDIM, HDIM), HDIM)] = mixed.astype(jnp.bfloat16)
+                return carry
+
+            lax.fori_loop(0, group_size, one, 0)
+
+        part(1 - core, msend.at[h])
+        mix_copy(h).start()
+        part(core, mix.at[h, 0])
+
+    def mix_copy(h):
+        return remote(msend.at[h], mix.at[h, 1], psem.at[h], prsem.at[h], dev_core)
+
+    def product(h, side, cols):
+        return jnp.dot(mix[h, side], wbuf[h % 2, side, :, cols], preferred_element_type=jnp.float32)
+
+    def weights(h):
+        for side in (0, 1):
+            owner = core + side * (1 - 2 * core)
+            wrows = pl.ds(pl.multiple_of((owner * heads + h) * gwidth, gwidth), gwidth)
+            yield pltpu.make_async_copy(w_hbm.at[wrows, :], wbuf.at[h % 2, side], wsem.at[h, side])
+
+    def fetch(h):
+        for c in weights(h):
+            c.start()
+
+    def fetched(h):
+        for c in weights(h):
+            c.wait()
+
+    def tile_cols(i):
+        return pl.ds(pl.multiple_of(i * TILE, TILE), TILE)
+
+    def project(h):
+        mix_copy(h).wait_recv()
+        fetched(h)
+
+        def one(i, carry):
+            cols = tile_cols(i)
+            pown[:, cols] += product(h, 0, cols) + product(h, 1, cols)
             return carry
 
-        lax.fori_loop(0, group_size, one, 0)
+        lax.fori_loop(0, tiles, one, 0)
+        when_head(h + 2, fetch)
+
+    def project_last(h):
+        fetched(h)
+
+        def one(i, carry):
+            cols = tile_cols(i)
+            pown[:, cols] += product(h, 0, cols)
+            return carry
+
+        lax.fori_loop(0, tiles, one, 0)
+        mix_copy(h).wait_recv()
+
+        def two(i, carry):
+            cols = tile_cols(i)
+            out_ref[:, cols] = (pown[:, cols] + product(h, 1, cols)).astype(jnp.bfloat16)
+            return carry
+
+        lax.fori_loop(0, tiles, two, 0)
 
     mine = pl.ds(pl.multiple_of(core * rows, rows), rows)
     hbms = (k_hbm, v_hbm)
@@ -248,9 +303,6 @@
     swaps.append(remote(
         q_hbm.at[:, half_cols(1 - core)], qbuf.at[mine, :],
         xsend.at[2 * heads], xrecv.at[2 * heads], dev_core))
-    weights = pltpu.make_async_copy(
-        w_hbm.at[pl.ds(pl.multiple_of(core * qwidth, qwidth), qwidth), :], wbuf,
-        local_sem.at[2 * heads + 1])
 
     for c in local:
         c.start()
@@ -279,13 +331,16 @@
 
     for c in swaps:
         c.start()
-    weights.start()
-    for c in local:
-        c.wait()
-    for c in swaps:
-        c.wait_recv()
-
-    event_0(0)
+
+    def own_ready(h):
+        for i in (2 * h, 2 * h + 1):
+            local[i].wait()
+            swaps[i].wait_recv()
+
+    own_ready(0)
+    start(ZB, 0)
+    for h in range(1, heads):
+        own_ready(h)
     for h in range(heads):
         cols = slice(h * HDIM, (h + 1) * HDIM)
         kf = feature(kbuf[h, j]).astype(jnp.bfloat16)
@@ -295,21 +350,38 @@
         norm = jnp.sum(kf.astype(jnp.float32), axis=0, keepdims=True)
         dsum[HDIM:, cols] = jnp.broadcast_to(norm, (PAD, HDIM))
     delta_send(0, dsum[...])
-    event_1(0)
-    event_0(1)
-    dsum[...] += delta_arrive(0)
-    delta_send(1, dsum[...])
-    event_2(0)
-    event_3(0)
-    other = delta_arrive(1)
-    dpre[...] = other * ybit.astype(jnp.float32)
-    dsum[...] += other
-
-    @pl.when(has_up & (plane == 0))
-    def _():
-        delta_send(2, dsum[...])
-
-    event_4(0)
+    start(AY, 0, ybit == 0)
+    start(AX, 0, xbit == 0)
+    local[2 * heads].wait()
+    swaps[2 * heads].wait_recv()
+    for h in range(min(2, heads)):
+        fetch(h)
+    pown[...] = jnp.zeros(pown.shape, jnp.float32)
+    def first_forward():
+        for kv in KV:
+            arrive(ZB, 0, (kv,))
+            start(ZC, 0, None, (kv,))
+            start(BX, 0, None, (kv,))
+            start(BY, 0, None, (kv,))
+        if heads > 1:
+            start(ZB, 1)
+        dsum[...] += delta_arrive(0)
+        delta_send(1, dsum[...])
+
+    def first_old():
+        for kv in KV:
+            arrive(ZC, 0, (kv,))
+            start(AY, 0, ybit == 1, (kv,))
+            start(AX, 0, xbit == 1, (kv,))
+
+    def first_plane():
+        other = delta_arrive(1)
+        dpre[...] = other * ybit.astype(jnp.float32)
+        dsum[...] += other
+
+        @pl.when(has_up & (plane == 0))
+        def _():
+            delta_send(2, dsum[...])
 
     def chain():
         @pl.when(has_down)
@@ -324,92 +396,122 @@
     def xor(a_bit, b_bit):
         return a_bit + b_bit - 2 * a_bit * b_bit
 
+    def one_of(s, *steps):
+        found = s == steps[0]
+        for k in steps[1:]:
+            found = found | (s == k)
+        return found
+
+    last_chain = 12
+
     def one_head(h, carry):
-        attend(h, j, "own")
-        when_head(h + 1, event_1)
+        attend(h, (j,), "own")
+
+        @pl.when(h == 0)
+        def _():
+            first_forward()
+
+        def look_ahead():
+            @pl.when(h + 1 < heads)
+            def _():
+                relay(ZB, ZC, h + 1)
+
+            @pl.when(h + 2 < heads)
+            def _():
+                start(ZB, h + 2)
 
         def step(s, c):
-            late = s // 4
-            t = s - 3 * late
-            slot = 4 * (1 - late) + xor(xbit, t % 2) + 2 * xor(ybit, t // 2)
+            old = one_of(s, 2, 3, 5)
+
+            def slot_of(k):
+                flip_x = jnp.where(one_of(k, 1, 3, 5, 6), 1, 0)
+                flip_y = jnp.where(one_of(k, 2, 4, 5, 6), 1, 0)
+                return jnp.where(one_of(k, 2, 3, 5), 0, 4) + xor(xbit, flip_x) + 2 * xor(ybit, flip_y)
 
             @pl.when(s == 1)
             def _():
-                when_head(h + 2, event_0)
-
-            @pl.when(s == 2)
-            def _():
-                arrive(BY, h)
-
-            @pl.when(s == 3)
-            def _():
-                when_head(h + 1, event_2)
-                when_head(h + 1, event_3)
-                arrive(BYF, h)
-
                 @pl.when(h == 0)
                 def _():
-                    chain()
+                    first_old()
+
+                look_ahead()
+
+                @pl.when(two_down)
+                def _():
+                    attend(h, (8,), "old")
+
+                relay(BX, BYF, h)
+
+            @pl.when(s == 2)
+            def _():
+                relay(AY, AXF, h)
+
+                @pl.when(h == 0)
+                def _():
+                    first_plane()
+
+            @pl.when(s == 3)
+            def _():
+                when_head(h + 1, open_head)
+
+                @pl.when(h == 2)
+                def _():
+                    project(0)
+
+                arrive(AX, h)
 
             @pl.when(s == 4)
             def _():
-                arrive(AX, h)
+                arrive(BY, h)
 
             @pl.when(s == 5)
             def _():
-                when_head(h + 1, event_4)
+                arrive(AXF, h)
 
             @pl.when(s == 6)
             def _():
-                arrive(AXF, h)
-
-            bit = jnp.where(s == 4, xbit, ybit)
-            valid = ((s < 4) & has_down) | ((s >= 4) & ((bit == 1) | two_down))
-
-            @pl.when(valid)
-            def _():
-                attend(h, slot)
+                arrive(BYF, h)
+
+            @pl.when(7 * h + s == jnp.minimum(4 * plane, last_chain))
+            def _():
+                chain()
+
+            @pl.when((h > 0) & (s == jnp.where(h == 1, 6, 2)))
+            def _():
+                finish(h - 1)
+
+            @pl.when((h > 1) & (s == 6))
+            def _():
+                project(h - 1)
+
+            bit = jnp.where(s == 3, xbit, ybit)
+            held = jnp.where(old, jnp.where(bit == 1, 1, 0), jnp.where(has_down, 1, 0))
+            alone = jnp.where(two_down, jnp.where(s == 0, 1, 0), held)
+
+            @pl.when(alone == 1)
+            def _():
+                attend(h, (slot_of(s),))
+
+            @pl.when(two_down & one_of(s, 2, 4, 6))
+            def _():
+                attend(h, (slot_of(s - 1), slot_of(s)))
 
             return c
 
         lax.fori_loop(0, 7, step, 0)
-
-        @pl.when(two_down)
-        def _():
-            attend(h, 8, "old")
-
-        finish(h)
         return carry
 
     lax.fori_loop(0, heads, one_head, 0)
-
-    weights.wait()
-    theirs = pl.ds(pl.multiple_of((1 - core) * rows, rows), rows)
-
-    def partial_copy(i):
-        return remote(psend.at[i], precv.at[i], psem.at[i], prsem.at[i], dev_core)
-
-    def project(i, carry):
-        cols = pl.ds(pl.multiple_of(i * TILE, TILE), TILE)
-        psend[i] = jnp.dot(mix[theirs, :], wbuf[:, cols], preferred_element_type=jnp.float32)
-        partial_copy(i).start()
+    if heads == 2:
+        project(0)
+    finish(heads - 1)
+    project_last(heads - 1)
+
+    def sent(h, carry):
+        mix_copy(h).wait_send()
         return carry
 
-    def project_own(i, carry):
-        cols = pl.ds(pl.multiple_of(i * TILE, TILE), TILE)
-        pown[...] = jnp.dot(mix[mine, :], wbuf[:, cols], preferred_element_type=jnp.float32)
-        partial_copy(i).wait_recv()
-        out_ref[:, cols] = (pown[...] + precv[i]).astype(jnp.bfloat16)
-        return carry
-
-    lax.fori_loop(0, tiles, project, 0)
-    lax.fori_loop(0, tiles, project_own, 0)
-
-    def sent(i, carry):
-        partial_copy(i).wait_send()
-        return carry
-
-    lax.fori_loop(0, tiles, sent, 0)
+    lax.fori_loop(0, heads, sent, 0)
     for c in swaps:
         c.wait_send()
     for i in (0, 1):
@@ -435,11 +537,10 @@
     heads = gate_logit.shape[0]
     groups = keys.shape[1] // HDIM
     group_size = heads // groups
-    assert WINDOW == 16 * rows and SEG == 4 * rows and size % 8 == 0 and groups % 2 == 0
+    assert WINDOW == 16 * rows and SEG == 4 * rows and size % 8 == 0 and groups % 2 == 0 and groups >= 4
     mine = groups // 2
     columns = out_weight.shape[1]
     qwidth = mine * group_size * HDIM
-    tiles = columns // TILE
     f32, bf16 = jnp.float32, jnp.bfloat16
     vmem, anywhere = pl.BlockSpec(memory_space=pltpu.VMEM), pl.BlockSpec(memory_space=pl.ANY)
     dma = pltpu.SemaphoreType.DMA
@@ -453,30 +554,30 @@
             pltpu.VMEM((mine, 9, 2 * rows, HDIM), bf16),
             pltpu.VMEM((mine, 9, 2 * rows, HDIM), bf16),
             pltpu.VMEM((2 * rows * group_size, HDIM), f32),
-            pltpu.VMEM((2 * rows * group_size, 2 * HDIM), f32),
-            pltpu.VMEM((2 * rows, qwidth), bf16),
-            pltpu.VMEM((qwidth, columns), bf16),
-            pltpu.VMEM((tiles, rows, TILE), f32),
-            pltpu.VMEM((tiles, rows, TILE), f32),
-            pltpu.VMEM((rows, TILE), f32),
+            pltpu.VMEM((2, 2 * rows * group_size, 2 * HDIM), f32),
+            pltpu.VMEM((mine, 2, rows, group_size * HDIM), bf16),
+            pltpu.VMEM((mine, rows, group_size * HDIM), bf16),
+            pltpu.VMEM((2, 2, group_size * HDIM, columns), bf16),
+            pltpu.VMEM((rows, columns), f32),
             pltpu.VMEM((3, HDIM + PAD, mine * HDIM), bf16),
             pltpu.VMEM((3, HDIM + PAD, mine * HDIM), bf16),
             pltpu.VMEM((HDIM + PAD, mine * HDIM), f32),
             pltpu.VMEM((HDIM + PAD, mine * HDIM), f32),
-            dma((2 * mine + 2,)),
+            dma((2 * mine + 1,)),
             dma((2 * mine + 1,)),
             dma((2 * mine + 1,)),
             dma((8, mine, 2)),
             dma((8, mine, 2)),
             dma((3,)),
             dma((3,)),
-            dma((tiles,)),
-            dma((tiles,)),
+            dma((mine,)),
+            dma((mine,)),
+            dma((mine, 2)),
         ],
         compiler_params=pltpu.CompilerParams(
             collective_id=0, has_side_effects=True, vmem_limit_bytes=60 * 1024 * 1024
         ),
-    )(jax.nn.sigmoid(gate_logit), queries, keys, values, out_weight)
+    )(gate_logit, queries, keys, values, out_weight)
     return lax.psum_scatter(partial_value, "head", scatter_dimension=1, tiled=True)
 
 

time: 132 us -> 106 us (0.80)
  Pallas kernels: 127 us -> 103 us
    pallas_call x1, Pallas kernels: 127 us -> 103 us  [per_device(): pl.pallas_call(functools.partial(kernel, size, group_size), out_shape=jax...]
where the time goes in v2:
time: 106 us
  Pallas kernels  103 us (97%)
  local copies, waits for them, and re-layouts  3.13 us (3%)
    pallas_call x1, Pallas kernels, per_device(): pl.pallas_call(functools.partial(kernel, size, group_size), out_shape=jax...  103 us
    unnamed x1, local copies, waits for them, and re-layouts  3.13 us

profile of v2, /device:TPU:24, one launch (start us, length us, event | category | flops | bytes accessed | tf_op | source)
XLA Modules:
  0.0 106.2 jit_solution(17731327245352461786)
XLA Ops:
  0.0 103.1 %shard_map.55 = bf16[256,4096]{1,0:T(8,128)(2,1)} custom-call(f32[32]{0:T(128)} %gate_ref.1, bf16[256,4096]{1,0:T(8,128)(2,1)} %q_hbm.1, bf16[256,1024]{1,0:T(8,128)(2,1)} %k_hbm.1, bf16[256,1024]{1,0:T(8,128)(2,1)} %v_hbm.1, bf16[4096,4096]{1,0:T(8,128)(2,1)} %w_hbm.1), custom_call_target="tpu_custom_call" | custom-call | tf_op jit(solution)/shard_map/pallas_call | solution.py:547
  103.1 3.1 %copy.7 = bf16[256,4096]{1,0:T(8,128)(2,1)} copy(bf16[256,4096]{1,0:T(8,128)(2,1)} %shard_map.55) | data formatting | bytes 4194304

commit v3 on v2

--- a/solution.py
+++ b/solution.py
@@ -13,7 +13,7 @@
 SEG = 1024
 LOG2E = 1.4426950408889634
 EXP_SCALE = LOG2E / math.sqrt(HDIM)
-TILE = 1024
+TILE = 2048
 PAD = 16
 ZB, ZC, BX, BY, BYF, AX, AY, AXF = range(8)
 KV = (0, 1)
@@ -221,7 +221,7 @@
                 target[:, pl.ds(pl.multiple_of(r * HDIM, HDIM), HDIM)] = mixed.astype(jnp.bfloat16)
                 return carry
 
-            lax.fori_loop(0, group_size, one, 0)
+            lax.fori_loop(0, group_size, one, 0, unroll=True)
 
         part(1 - core, msend.at[h])
         mix_copy(h).start()
@@ -411,14 +411,14 @@
         def _():
             first_forward()
 
-        def look_ahead():
-            @pl.when(h + 1 < heads)
-            def _():
-                relay(ZB, ZC, h + 1)
-
-            @pl.when(h + 2 < heads)
-            def _():
-                start(ZB, h + 2)
+        def look_ahead(k):
+            @pl.when(k < heads)
+            def _():
+                relay(ZB, ZC, k)
+
+            @pl.when(k + 1 < heads)
+            def _():
+                start(ZB, k + 1)
 
         def step(s, c):
             old = one_of(s, 2, 3, 5)
@@ -433,8 +433,7 @@
                 @pl.when(h == 0)
                 def _():
                     first_old()
-
-                look_ahead()
+                    look_ahead(1)
 
                 @pl.when(two_down)
                 def _():
@@ -466,6 +465,7 @@
 
             @pl.when(s == 5)
             def _():
+                look_ahead(h + 2)
                 arrive(AXF, h)
 
             @pl.when(s == 6)

time: 106 us -> 98.7 us (0.931)
  Pallas kernels: 103 us -> 95.4 us
    pallas_call x1, Pallas kernels: 103 us -> 95.4 us  [per_device(): pl.pallas_call(functools.partial(kernel, size, group_size), out_shape=jax...]
where the time goes in v3:
time: 98.7 us; the launch traced here: 98.5 us
  Pallas kernels  95.4 us (97%)
  local copies, waits for them, and re-layouts  3.13 us (3%)
    pallas_call x1, Pallas kernels, per_device(): pl.pallas_call(functools.partial(kernel, size, group_size), out_shape=jax...  95.4 us
    unnamed x1, local copies, waits for them, and re-layouts  3.13 us

profile of v3, /device:TPU:24, one launch (start us, length us, event | category | flops | bytes accessed | tf_op | source)
XLA Modules:
  0.0 98.5 jit_solution(3461737008124774793)
XLA Ops:
  0.0 95.4 %shard_map.55 = bf16[256,4096]{1,0:T(8,128)(2,1)} custom-call(f32[32]{0:T(128)} %gate_ref.1, bf16[256,4096]{1,0:T(8,128)(2,1)} %q_hbm.1, bf16[256,1024]{1,0:T(8,128)(2,1)} %k_hbm.1, bf16[256,1024]{1,0:T(8,128)(2,1)} %v_hbm.1, bf16[4096,4096]{1,0:T(8,128)(2,1)} %w_hbm.1), custom_call_target="tpu_custom_call" | custom-call | tf_op jit(solution)/shard_map/pallas_call | solution.py:547
  95.4 3.1 %copy.7 = bf16[256,4096]{1,0:T(8,128)(2,1)} copy(bf16[256,4096]{1,0:T(8,128)(2,1)} %shard_map.55) | data formatting | bytes 4194304
